TPU v7x, 32 devices: a whole 2x2x4 slice. The times are simulated.
32 devices in a mesh: dp: 4 (over x, core), hist: 8 (over z, y).
Axes of the slice: x: 2, y: 2, z: 4, core: 2. Of those that a mesh axis runs over, the one named last changes fastest.
Arguments:
- candidates: bfloat16 [16, 512, 128], P('dp', 'hist'), may hold values from -150 to 150
- history: bfloat16 [16, 16384, 128], P('dp', 'hist'), may hold values from -6 to 6
- projections: bfloat16 [4, 128, 128], P(None, 'dp'), may hold values from -0.5 to 0.5
- lengths: int32 [16], P('dp'), may hold values from 8193 to 16384
- selected: int32 [16, 64], P('dp'), may hold values from 0 to 127, as said below
Outputs:
- interest: bfloat16 [16, 512, 128], P('dp', 'hist')
Inputs may be any that keep to these rules, and one draw needn't show every extreme that they name: `selected`: each row names 64 different history blocks.
All inputs are finite; a program needn't handle non-finite values.
Results may differ from a plain program's by a relative error of at most 0.008.
The roundings to bfloat16 on the way count: a program that leaves them out, or rounds other values in their place, can miss the bound.
Values may be sent and summed in bfloat16 or wider, within the bound.
A program may use at most 128 MiB of HBM per device.

v0:
```python
import math
import jax
import jax.numpy as jnp
from jax import lax
from jax.sharding import PartitionSpec as P

D = 128
H = 4
BLOCK = 128


def scale_heads(blocks, factor):
    layout = blocks.shape
    heads = factor.shape[-1]
    return (blocks.reshape(layout[:-1] + (heads, layout[-1] // heads)) * factor[..., None]).reshape(
        layout
    )


def body(candidates, history, projections, lengths, selected):
    weights = lax.all_gather(projections, "dp", axis=1, tiled=True)
    user_count, own_cands, embed = candidates.shape
    head_size = D // H
    inv_root = 1.0 / math.sqrt(head_size)
    whole = lax.all_gather(candidates, "hist", axis=1, tiled=True)
    queries = jnp.dot(whole.reshape(-1, embed), weights[0], preferred_element_type=jnp.float32)
    queries = queries.astype(jnp.bfloat16).reshape(user_count, -1, embed)
    cand_count = queries.shape[1]
    own_rows = history.shape[1]
    key_value = jnp.concatenate([weights[1], weights[2]], axis=1)
    projected = jnp.dot(history.reshape(-1, embed), key_value, preferred_element_type=jnp.float32)
    projected = projected.astype(jnp.bfloat16).reshape(user_count, own_rows, 2 * embed)
    keys = projected[:, :, :embed]
    values = projected[:, :, embed:]
    places = lax.axis_index("hist") * own_rows + jnp.arange(own_rows, dtype=jnp.int32)
    block_ids = places // BLOCK
    chosen = jnp.any(selected[:, :, None] == block_ids[None, None, :], axis=1)
    live = jnp.logical_and(chosen, places[None, :] < lengths[:, None])
    span = min(512, own_rows)
    pieces = own_rows // span

    def attend(item):
        query_rows, key_rows, value_rows, live_row = item
        query_heads = query_rows.reshape(cand_count, H, head_size)

        def one_piece(sub):
            key_part, value_part, live_part = sub
            scores = (
                jnp.einsum(
                    "chd,khd->hck",
                    query_heads,
                    key_part.reshape(span, H, head_size),
                    preferred_element_type=jnp.float32,
                )
                * inv_root
            )
            scores = jnp.where(live_part[None, None, :], scores, -1e30)
            maxima = jnp.max(scores, axis=-1)
            expo = jnp.where(live_part[None, None, :], jnp.exp(scores - maxima[:, :, None]), 0.0)
            totals = jnp.sum(expo, axis=-1)
            summed = jnp.einsum(
                "hck,khd->chd",
                expo.astype(jnp.bfloat16),
                value_part.reshape(span, H, head_size),
                preferred_element_type=jnp.float32,
            )
            return (maxima.T, totals.T, summed.reshape(cand_count, embed))

        maxima_all, totals_all, summed_all = lax.map(
            one_piece,
            (
                key_rows.reshape(pieces, span, embed),
                value_rows.reshape(pieces, span, embed),
                live_row.reshape(pieces, span),
            ),
        )
        highest = jnp.max(maxima_all, axis=0)
        factors = jnp.exp(maxima_all - highest[None])
        totals = jnp.sum(totals_all * factors, axis=0)
        summed = jnp.sum(scale_heads(summed_all, factors), axis=0)
        return (highest, totals, summed)

    def per_user(item):
        return attend(item)

    maxima, totals, summed = lax.map(per_user, (queries, keys, values, live))
    maxima_all, totals_all, summed_all = (
        lax.all_to_all(maxima[None], "hist", split_axis=2, concat_axis=0, tiled=True),
        lax.all_to_all(totals[None], "hist", split_axis=2, concat_axis=0, tiled=True),
        lax.all_to_all(summed[None], "hist", split_axis=2, concat_axis=0, tiled=True),
    )
    highest = jnp.max(maxima_all, axis=0)
    factors = jnp.exp(maxima_all - highest[None])
    totals = jnp.sum(totals_all * factors, axis=0)
    summed = jnp.sum(scale_heads(summed_all, factors), axis=0)
    attended = scale_heads(summed, 1.0 / totals).astype(jnp.bfloat16)
    interest = jnp.dot(attended.reshape(-1, embed), weights[3], preferred_element_type=jnp.float32)
    return interest.astype(jnp.bfloat16).reshape(user_count, own_cands, embed)


def solution(mesh):
    placed = (
        P("dp", "hist", None),
        P("dp", "hist", None),
        P(None, "dp", None),
        P("dp"),
        P("dp", None),
    )
    return jax.shard_map(
        body, mesh=mesh, in_specs=placed, out_specs=P("dp", "hist", None), check_vma=False
    )
```

profile of v0, /device:TPU:0, one launch (start us, length us, event | category | flops | bytes accessed | tf_op | source)
XLA Modules:
  0.0 321.4 jit_solution(1402405281978077282)
XLA Ops:
  0.0 6.9 %all_gather.6 = bf16[4,128,128]{2,1,0:T(8,128)(2,1)S(1)} all-gather(bf16[4,32,128]{2,1,0:T(8,128)(2,1)} %param.11), channel_id=1, replica_groups=mesh['dp'=4,'hist'=8] {'dp'}, dimensions={1}, use_global_device_ids=true | all-gather | bytes 163840 | tf_op jit(solution)/shard_map/all_gather | solution.py:21
  6.9 3.2 %fusion.12 = bf16[8192,256]{0,1:T(8,128)(2,1)} fusion(bf16[8192,128]{1,0:T(8,128)(2,1)S(1)} %bitcast.121, bf16[128,128]{1,0:T(8,128)(2,1)S(1)} %get-tuple-element.245, bf16[128,128]{1,0:T(8,128)(2,1)S(1)} %get-tuple-element.244), kind=kOutput, calls=%fused_computation.30 | convolution fusion | flops 539099136 | bytes 6356992 | tf_op jit(solution)/shard_map/dot_general | solution.py:31
  10.2 6.4 %copy.83 = bf16[8192,256]{1,0:T(8,128)(2,1)} copy(bf16[8192,256]{0,1:T(8,128)(2,1)} %fusion.12) | data formatting | bytes 8388608 | tf_op jit(solution)/shard_map/reshape | solution.py:32
  16.6 4.5 %fusion.20 = (bf16[4,2048,128]{2,1,0:T(8,128)(2,1)}, bf16[4,2048,128]{2,1,0:T(8,128)(2,1)}) fusion(bf16[4,2048,256]{2,1,0:T(8,128)(2,1)} %bitcast.129), kind=kLoop, calls=%fused_computation.57 | loop fusion | bytes 8388608 | tf_op jit(solution)/shard_map/slice | solution.py:34
  21.1 32.3 %all_gather.7 = bf16[4,512,128]{2,1,0:T(8,128)(2,1)S(1)} all-gather(bf16[4,64,128]{2,1,0:T(8,128)(2,1)S(1)} %copy-done.3), channel_id=1, replica_groups=mesh['dp'=4,'hist'=8] {'hist'}, dimensions={1}, use_global_device_ids=true | all-gather | bytes 589824 | tf_op jit(solution)/shard_map/all_gather | solution.py:25
  55.6 207.6 %while.29 = (s32[]{:T(128)}, f32[4,512,4]{1,2,0:T(4,128)}, f32[4,512,4]{1,2,0:T(4,128)}, f32[4,512,128]{2,0,1:T(4,128)}, bf16[4,2048,128]{2,1,0:T(8,128)(2,1)}, ...) while((s32[]{:T(128)}, f32[4,512,4]{1,2,0:T(4,128)}, ...), condition=%wide.region_9.10_spmd, body=%wide.region_1.9_spmd.sunk | while | flops 148332544 | bytes 36866940 | solution.py:86
  59.5 36.4 %while.30 = (s32[]{:T(128)}, f32[4,512,4]{1,2,0:T(4,128)}, f32[4,512,4]{1,2,0:T(4,128)}, f32[4,512,128]{1,2,0:T(8,128)}, pred[4,512]{1,0:T(4,128)(4,1)S(1)}, /*i...) while((s32[]{:T(128)}, f32[4,512,4]{1,2,0:T(4,128)}, ...), condition=%wide.region_5.5_spmd, body=%wide.region_2.4_spmd.sunk | while | flops 147845120 | bytes 31656596 | solution.py:69
  64.7 3.2 %fusion.40 = f32[4,32,512]{2,1,0:T(8,128)S(1)} fusion(bf16[512,4,32]{0,2,1:T(8,128)(2,1)S(1)} %bitcast.125, f32[4,512,512]{2,1,0:T(8,128)} %copy-done.1, f32[4,512]{1,0:T(4,128)S(1)} %get-tuple-element.380, pred[512]{0:T(512)(128)(4,1)S(1)} %dynamic-slice_reduce_fusion.5), kind=kOutput, calls=%fused_computation.7.clone.1 | convolution fusion | flops 72351744 | bytes 4596224 | tf_op jit(solution)/shard_map/while/body/eval_jaxpr/while/body/eval_jaxpr/hck,khd->chd/dot_general | solution.py:61
  73.7 3.2 %fusion.40 = f32[4,32,512]{2,1,0:T(8,128)S(1)} fusion(bf16[512,4,32]{0,2,1:T(8,128)(2,1)S(1)} %bitcast.125, f32[4,512,512]{2,1,0:T(8,128)} %copy-done.1, f32[4,512]{1,0:T(4,128)S(1)} %get-tuple-element.380, pred[512]{0:T(512)(128)(4,1)S(1)} %dynamic-slice_reduce_fusion.5), kind=kOutput, calls=%fused_computation.7.clone.1 | convolution fusion | flops 72351744 | bytes 4596224 | tf_op jit(solution)/shard_map/while/body/eval_jaxpr/while/body/eval_jaxpr/hck,khd->chd/dot_general | solution.py:61
  82.8 3.2 %fusion.40 = f32[4,32,512]{2,1,0:T(8,128)S(1)} fusion(bf16[512,4,32]{0,2,1:T(8,128)(2,1)S(1)} %bitcast.125, f32[4,512,512]{2,1,0:T(8,128)} %copy-done.1, f32[4,512]{1,0:T(4,128)S(1)} %get-tuple-element.380, pred[512]{0:T(512)(128)(4,1)S(1)} %dynamic-slice_reduce_fusion.5), kind=kOutput, calls=%fused_computation.7.clone.1 | convolution fusion | flops 72351744 | bytes 4596224 | tf_op jit(solution)/shard_map/while/body/eval_jaxpr/while/body/eval_jaxpr/hck,khd->chd/dot_general | solution.py:61
  91.9 3.2 %fusion.40 = f32[4,32,512]{2,1,0:T(8,128)S(1)} fusion(bf16[512,4,32]{0,2,1:T(8,128)(2,1)S(1)} %bitcast.125, f32[4,512,512]{2,1,0:T(8,128)} %copy-done.1, f32[4,512]{1,0:T(4,128)S(1)} %get-tuple-element.380, pred[512]{0:T(512)(128)(4,1)S(1)} %dynamic-slice_reduce_fusion.5), kind=kOutput, calls=%fused_computation.7.clone.1 | convolution fusion | flops 72351744 | bytes 4596224 | tf_op jit(solution)/shard_map/while/body/eval_jaxpr/while/body/eval_jaxpr/hck,khd->chd/dot_general | solution.py:61
  99.6 7.9 %dynamic_update_slice.30 = f32[4,512,128]{2,0,1:T(4,128)} dynamic-update-slice(f32[4,512,128]{2,0,1:T(4,128)} %get-tuple-element.425, f32[1,512,128]{2,0,1:T(1,128)S(1)} %copy.96, s32[]{:T(128)S(6)} %copy.121, s32[]{:T(128)} %constant.66.clone.1..sunk, s32[]{:T(128)} %constant.66.clone.1..sunk) | dynamic-update-slice | bytes 524292 | tf_op jit(solution)/shard_map/while/body/jit(dynamic_update_index_in_dim)/dynamic_update_slice | solution.py:86
  111.4 36.4 %while.30 = (s32[]{:T(128)}, f32[4,512,4]{1,2,0:T(4,128)}, f32[4,512,4]{1,2,0:T(4,128)}, f32[4,512,128]{1,2,0:T(8,128)}, pred[4,512]{1,0:T(4,128)(4,1)S(1)}, /*i...) while((s32[]{:T(128)}, f32[4,512,4]{1,2,0:T(4,128)}, ...), condition=%wide.region_5.5_spmd, body=%wide.region_2.4_spmd.sunk | while | flops 147845120 | bytes 31656596 | solution.py:69
  143.8 3.2 %fusion.40 = f32[4,32,512]{2,1,0:T(8,128)S(1)} fusion(bf16[512,4,32]{0,2,1:T(8,128)(2,1)S(1)} %bitcast.125, f32[4,512,512]{2,1,0:T(8,128)} %copy-done.1, f32[4,512]{1,0:T(4,128)S(1)} %get-tuple-element.380, pred[512]{0:T(512)(128)(4,1)S(1)} %dynamic-slice_reduce_fusion.5), kind=kOutput, calls=%fused_computation.7.clone.1 | convolution fusion | flops 72351744 | bytes 4596224 | tf_op jit(solution)/shard_map/while/body/eval_jaxpr/while/body/eval_jaxpr/hck,khd->chd/dot_general | solution.py:61
  151.5 7.9 %dynamic_update_slice.30 = f32[4,512,128]{2,0,1:T(4,128)} dynamic-update-slice(f32[4,512,128]{2,0,1:T(4,128)} %get-tuple-element.425, f32[1,512,128]{2,0,1:T(1,128)S(1)} %copy.96, s32[]{:T(128)S(6)} %copy.121, s32[]{:T(128)} %constant.66.clone.1..sunk, s32[]{:T(128)} %constant.66.clone.1..sunk) | dynamic-update-slice | bytes 524292 | tf_op jit(solution)/shard_map/while/body/jit(dynamic_update_index_in_dim)/dynamic_update_slice | solution.py:86
  163.3 36.4 %while.30 = (s32[]{:T(128)}, f32[4,512,4]{1,2,0:T(4,128)}, f32[4,512,4]{1,2,0:T(4,128)}, f32[4,512,128]{1,2,0:T(8,128)}, pred[4,512]{1,0:T(4,128)(4,1)S(1)}, /*i...) while((s32[]{:T(128)}, f32[4,512,4]{1,2,0:T(4,128)}, ...), condition=%wide.region_5.5_spmd, body=%wide.region_2.4_spmd.sunk | while | flops 147845120 | bytes 31656596 | solution.py:69
  177.5 3.2 %fusion.40 = f32[4,32,512]{2,1,0:T(8,128)S(1)} fusion(bf16[512,4,32]{0,2,1:T(8,128)(2,1)S(1)} %bitcast.125, f32[4,512,512]{2,1,0:T(8,128)} %copy-done.1, f32[4,512]{1,0:T(4,128)S(1)} %get-tuple-element.380, pred[512]{0:T(512)(128)(4,1)S(1)} %dynamic-slice_reduce_fusion.5), kind=kOutput, calls=%fused_computation.7.clone.1 | convolution fusion | flops 72351744 | bytes 4596224 | tf_op jit(solution)/shard_map/while/body/eval_jaxpr/while/body/eval_jaxpr/hck,khd->chd/dot_general | solution.py:61
  203.4 7.9 %dynamic_update_slice.30 = f32[4,512,128]{2,0,1:T(4,128)} dynamic-update-slice(f32[4,512,128]{2,0,1:T(4,128)} %get-tuple-element.425, f32[1,512,128]{2,0,1:T(1,128)S(1)} %copy.96, s32[]{:T(128)S(6)} %copy.121, s32[]{:T(128)} %constant.66.clone.1..sunk, s32[]{:T(128)} %constant.66.clone.1..sunk) | dynamic-update-slice | bytes 524292 | tf_op jit(solution)/shard_map/while/body/jit(dynamic_update_index_in_dim)/dynamic_update_slice | solution.py:86
  215.2 36.4 %while.30 = (s32[]{:T(128)}, f32[4,512,4]{1,2,0:T(4,128)}, f32[4,512,4]{1,2,0:T(4,128)}, f32[4,512,128]{1,2,0:T(8,128)}, pred[4,512]{1,0:T(4,128)(4,1)S(1)}, /*i...) while((s32[]{:T(128)}, f32[4,512,4]{1,2,0:T(4,128)}, ...), condition=%wide.region_5.5_spmd, body=%wide.region_2.4_spmd.sunk | while | flops 147845120 | bytes 31656596 | solution.py:69
  247.6 3.2 %fusion.40 = f32[4,32,512]{2,1,0:T(8,128)S(1)} fusion(bf16[512,4,32]{0,2,1:T(8,128)(2,1)S(1)} %bitcast.125, f32[4,512,512]{2,1,0:T(8,128)} %copy-done.1, f32[4,512]{1,0:T(4,128)S(1)} %get-tuple-element.380, pred[512]{0:T(512)(128)(4,1)S(1)} %dynamic-slice_reduce_fusion.5), kind=kOutput, calls=%fused_computation.7.clone.1 | convolution fusion | flops 72351744 | bytes 4596224 | tf_op jit(solution)/shard_map/while/body/eval_jaxpr/while/body/eval_jaxpr/hck,khd->chd/dot_general | solution.py:61
  255.3 7.9 %dynamic_update_slice.30 = f32[4,512,128]{2,0,1:T(4,128)} dynamic-update-slice(f32[4,512,128]{2,0,1:T(4,128)} %get-tuple-element.425, f32[1,512,128]{2,0,1:T(1,128)S(1)} %copy.96, s32[]{:T(128)S(6)} %copy.121, s32[]{:T(128)} %constant.66.clone.1..sunk, s32[]{:T(128)} %constant.66.clone.1..sunk) | dynamic-update-slice | bytes 524292 | tf_op jit(solution)/shard_map/while/body/jit(dynamic_update_index_in_dim)/dynamic_update_slice | solution.py:86
  270.5 5.3 %all-to-all-start.2 = ((f32[8,1,1024]{2,1,0:T(1,128)}), f32[8,1,1024]{2,1,0:T(1,128)S(1)}, u32[]{:S(2)}, u32[]{:S(2)}) async-start(f32[8,1,1024]{2,1,0:T(1,128)} %reshape.121), calls=%async_computation.2 | async-start | bytes 65536 | tf_op jit(solution)/shard_map/all_to_all | solution.py:89
  282.5 11.9 %all_to_all.51 = f32[8,1,1024]{2,1,0:T(1,128)S(1)} all-to-all(f32[8,1,1024]{2,1,0:T(1,128)S(1)} %reshape.119), channel_id=1, replica_groups=mesh['dp'=4,'hist'=8] {'hist'}, dimensions={0} | all-to-all | bytes 65536 | tf_op jit(solution)/shard_map/all_to_all | solution.py:88
  294.4 4.4 %all-to-all-start = ((f32[1,4,512,128]{3,1,0,2:T(4,128)}), f32[1,4,512,128]{3,1,0,2:T(4,128)}, u32[]{:S(2)}, u32[]{:S(2)}) async-start(f32[1,4,512,128]{3,1,0,2:T(4,128)} %bitcast.136), calls=%async_computation | async-start | bytes 2097152 | tf_op jit(solution)/shard_map/all_to_all | solution.py:90
  (288 shorter events, 191.4 us)
Async XLA Ops:
  0.0 6.9 %copy-start = (bf16[4,2048,128]{2,1,0:T(8,128)(2,1)S(1)}, bf16[4,2048,128]{2,1,0:T(8,128)(2,1)}, u32[]{:S(2)}) copy-start(bf16[4,2048,128]{2,1,0:T(8,128)(2,1)} %param.10) | copy-start | bytes 6291460
  6.9 46.5 %copy-start.2 = (bf16[4,128,128]{2,1,0:T(8,128)(2,1)}, bf16[4,128,128]{2,1,0:T(8,128)(2,1)S(1)}, u32[]{:S(2)}) copy-start(bf16[4,128,128]{2,1,0:T(8,128)(2,1)S(1)} %all_gather.6) | copy-start | bytes 393220
  16.6 4.5 %copy-start.3 = (bf16[4,64,128]{2,1,0:T(8,128)(2,1)S(1)}, bf16[4,64,128]{2,1,0:T(8,128)(2,1)}, u32[]{:S(2)}) copy-start(bf16[4,64,128]{2,1,0:T(8,128)(2,1)} %param.9) | copy-start | bytes 196612
  16.6 37.9 %copy-start.5 = (s32[4,64]{1,0:T(4,128)S(1)}, s32[4,64]{1,0:T(4,128)}, u32[]{:S(2)}) copy-start(s32[4,64]{1,0:T(4,128)} %param.13) | copy-start | bytes 3076
  16.6 38.3 %copy-start.6 = (s32[4]{0:T(128)S(1)}, s32[4]{0:T(128)}, u32[]{:S(2)}) copy-start(s32[4]{0:T(128)} %param.12) | copy-start | bytes 52
  60.8 1.9 copy-start.1
  69.9 1.9 copy-start.1
  79.0 1.9 copy-start.1
  88.1 1.9 copy-start.1
  112.7 1.9 copy-start.1
  121.8 1.9 copy-start.1
  130.9 1.9 copy-start.1
  140.0 1.9 copy-start.1
  164.6 1.9 copy-start.1
  173.7 1.9 copy-start.1
  182.8 1.9 copy-start.1
  191.9 1.9 copy-start.1
  216.5 1.9 copy-start.1
  225.6 1.9 copy-start.1
  234.7 1.9 copy-start.1
  243.8 1.9 copy-start.1
  263.1 12.7 %copy-start.4 = (f32[4,512,4]{1,2,0:T(4,128)S(1)}, f32[4,512,4]{1,2,0:T(4,128)}, u32[]{:S(2)}) copy-start(f32[4,512,4]{1,2,0:T(4,128)} %get-tuple-element.94) | copy-start | bytes 98308
  270.5 12.0 %all-to-all-start.2 = ((f32[8,1,1024]{2,1,0:T(1,128)}), f32[8,1,1024]{2,1,0:T(1,128)S(1)}, u32[]{:S(2)}, u32[]{:S(2)}) async-start(f32[8,1,1024]{2,1,0:T(1,128)} %reshape.121), calls=%async_computation.2 | async-start | bytes 65536 | tf_op jit(solution)/shard_map/all_to_all | solution.py:89
  294.4 22.8 %all-to-all-start = ((f32[1,4,512,128]{3,1,0,2:T(4,128)}), f32[1,4,512,128]{3,1,0,2:T(4,128)}, u32[]{:S(2)}, u32[]{:S(2)}) async-start(f32[1,4,512,128]{3,1,0,2:T(4,128)} %bitcast.136), calls=%async_computation | async-start | bytes 2097152 | tf_op jit(solution)/shard_map/all_to_all | solution.py:90
where the time goes:
time: 325 us; the launch traced here: 321 us
  local copies, waits for them, and re-layouts  144 us (44%)
  matrix products  75.4 us (23%)
  blocking collectives  51 us (16%)
  other arithmetic  38.9 us (12%)
  starting transfers between devices  9.74 us (3%)
    dynamic_update_slice x44, local copies, waits for them, and re-layouts, body(): maxima, totals, summed = lax.map(per_user, (queries, keys, values, live))  55.9 us
    dot_general x16, matrix products, one_piece(): jnp.einsum('hck,khd->chd', expo.astype(jnp.bfloat16), value_part.reshape(...  51.8 us
    all_gather x1, blocking collectives, body(): whole = lax.all_gather(candidates, 'hist', axis=1, tiled=True)  32.3 us
    while x32, local copies, waits for them, and re-layouts  30.7 us
    dynamic_slice x84, local copies, waits for them, and re-layouts, body(): maxima, totals, summed = lax.map(per_user, (queries, keys, values, live))  19.7 us
    reduce_sum x16, other arithmetic, one_piece(): totals = jnp.sum(expo, axis=-1)  18.6 us
    dot_general x16, matrix products, one_piece(): jnp.einsum('chd,khd->hck', query_heads, key_part.reshape(span, H, head_si...  17.7 us
    unnamed x18, local copies, waits for them, and re-layouts  14.6 us
  transfers between devices with their start and end apart: 2, of which 2 were waited for; matrix products, arithmetic and copies ran while one was open for 7% of the time, Pallas kernels for 0%

commit v1 on v0

--- a/solution.py
+++ b/solution.py
@@ -7,6 +7,16 @@
 D = 128
 H = 4
 BLOCK = 128
+
+
+def turned_line(x, axis, dim):
+    size = lax.axis_size(axis)
+    moving, blocks = (x, [x])
+    for _ in range(size - 1):
+        moving = lax.ppermute(moving, axis, [(i, (i + 1) % size) for i in range(size)])
+        blocks.insert(0, moving)
+    row_of_blocks = jnp.concatenate(blocks, axis=dim)
+    return jnp.roll(row_of_blocks, (lax.axis_index(axis) + 1) * x.shape[dim], axis=dim)
 
 
 def scale_heads(blocks, factor):
@@ -22,7 +32,7 @@
     user_count, own_cands, embed = candidates.shape
     head_size = D // H
     inv_root = 1.0 / math.sqrt(head_size)
-    whole = lax.all_gather(candidates, "hist", axis=1, tiled=True)
+    whole = turned_line(candidates, "hist", 1)
     queries = jnp.dot(whole.reshape(-1, embed), weights[0], preferred_element_type=jnp.float32)
     queries = queries.astype(jnp.bfloat16).reshape(user_count, -1, embed)
     cand_count = queries.shape[1]

time: 325 us -> 318 us (0.978)
  blocking collectives: 51 us -> 15.4 us
  waiting for transfers between devices: 1.26 us -> 34 us
  local copies, waits for them, and re-layouts: 144 us -> 138 us
  starting transfers between devices: 9.74 us -> 14.4 us
    all_gather x1 -> x0, blocking collectives: 32.3 us -> none  [body(): whole = lax.all_gather(candidates, 'hist', axis=1, tiled=True)]
    ppermute x0 -> x7, waiting for transfers between devices: none -> 27 us  [turned_line(): lax.ppermute(moving, axis, [(i, (i + 1) % size) for i in range(size)])]
    ppermute x0 -> x7, starting transfers between devices: none -> 6.7 us  [turned_line(): lax.ppermute(moving, axis, [(i, (i + 1) % size) for i in range(size)])]
    all_to_all x1, waiting for transfers between devices: 0.56 us -> 4.16 us  [body(): lax.all_to_all(summed[None], 'hist', split_axis=2, concat_axis=0, tiled=T...]
    unnamed x18 -> x33, local copies, waits for them, and re-layouts: 14.6 us -> 11.3 us
  transfers between devices with their start and end apart: 2 -> 9, of which waited for: 2 -> 7; matrix products, arithmetic and copies ran while one was open for 7% -> 11% of each run, Pallas kernels for 0% -> 0%
where the time goes in v1:
time: 318 us; the launch traced here: 315 us
  local copies, waits for them, and re-layouts  138 us (43%)
  matrix products  75.4 us (24%)
  other arithmetic  36.2 us (11%)
  waiting for transfers between devices  34 us (11%)
  blocking collectives  15.4 us (5%)
  starting transfers between devices  14.4 us (5%)
    dynamic_update_slice x44, local copies, waits for them, and re-layouts, body(): maxima, totals, summed = lax.map(per_user, (queries, keys, values, live))  56 us
    dot_general x16, matrix products, one_piece(): jnp.einsum('hck,khd->chd', expo.astype(jnp.bfloat16), value_part.reshape(...  51.8 us
    while x32, local copies, waits for them, and re-layouts  30.7 us
    ppermute x7, waiting for transfers between devices, turned_line(): lax.ppermute(moving, axis, [(i, (i + 1) % size) for i in range(size)])  27 us
    dynamic_slice x84, local copies, waits for them, and re-layouts, body(): maxima, totals, summed = lax.map(per_user, (queries, keys, values, live))  19.7 us
    reduce_sum x16, other arithmetic, one_piece(): totals = jnp.sum(expo, axis=-1)  18.6 us
    dot_general x16, matrix products, one_piece(): jnp.einsum('chd,khd->hck', query_heads, key_part.reshape(span, H, head_si...  17.8 us
    unnamed x33, local copies, waits for them, and re-layouts  11.3 us
  transfers between devices with their start and end apart: 9, of which 7 were waited for; matrix products, arithmetic and copies ran while one was open for 11% of the time, Pallas kernels for 0%

profile of v1, /device:TPU:0, one launch (start us, length us, event | category | flops | bytes accessed | tf_op | source)
XLA Modules:
  0.0 314.7 jit_solution(10333619185565211002)
XLA Ops:
  3.0 5.6 %all_gather.3 = bf16[4,128,128]{2,1,0:T(8,128)(2,1)S(1)} all-gather(bf16[4,32,128]{2,1,0:T(8,128)(2,1)} %param.11), channel_id=1, replica_groups=mesh['dp'=4,'hist'=8] {'dp'}, dimensions={1}, use_global_device_ids=true | all-gather | bytes 163840 | tf_op jit(solution)/shard_map/all_gather | solution.py:31
  10.2 3.3 %fusion.12 = bf16[8192,256]{0,1:T(8,128)(2,1)} fusion(bf16[8192,128]{1,0:T(8,128)(2,1)S(1)} %bitcast.121, bf16[128,128]{1,0:T(8,128)(2,1)S(1)} %get-tuple-element.245, bf16[128,128]{1,0:T(8,128)(2,1)S(1)} %get-tuple-element.244), kind=kOutput, calls=%fused_computation.30 | convolution fusion | flops 539099136 | bytes 6356992 | tf_op jit(solution)/shard_map/dot_general | solution.py:41
  13.5 6.4 %copy.83 = bf16[8192,256]{1,0:T(8,128)(2,1)} copy(bf16[8192,256]{0,1:T(8,128)(2,1)} %fusion.12) | data formatting | bytes 8388608 | tf_op jit(solution)/shard_map/reshape | solution.py:42
  21.4 4.5 %fusion.20 = (bf16[4,2048,128]{2,1,0:T(8,128)(2,1)}, bf16[4,2048,128]{2,1,0:T(8,128)(2,1)}) fusion(bf16[4,2048,256]{2,1,0:T(8,128)(2,1)} %bitcast.129), kind=kLoop, calls=%fused_computation.74 | loop fusion | bytes 8388608 | tf_op jit(solution)/shard_map/slice | solution.py:44
  27.4 6.3 %collective-permute-done.3 = bf16[4,64,128]{2,1,0:T(8,128)(2,1)S(1)} collective-permute-done((bf16[4,64,128]{2,1,0:T(8,128)(2,1)S(1)}, bf16[4,64,128]{2,1,0:T(8,128)(2,1)S(1)}, u32[]{:S(2)}, u32[]{:S(2)}) %collective-permute-start.3) | collective-permute-done | bytes 65568 | tf_op jit(solution)/shard_map/ppermute | solution.py:16
  34.2 6.6 %collective-permute-done.4 = bf16[4,64,128]{2,1,0:T(8,128)(2,1)S(1)} collective-permute-done((bf16[4,64,128]{2,1,0:T(8,128)(2,1)S(1)}, bf16[4,64,128]{2,1,0:T(8,128)(2,1)S(1)}, u32[]{:S(2)}, u32[]{:S(2)}) %collective-permute-start.4) | collective-permute-done | bytes 65568 | tf_op jit(solution)/shard_map/ppermute | solution.py:16
  40.8 7.0 %collective-permute-done.5 = bf16[4,64,128]{2,1,0:T(8,128)(2,1)S(1)} collective-permute-done((bf16[4,64,128]{2,1,0:T(8,128)(2,1)S(1)}, bf16[4,64,128]{2,1,0:T(8,128)(2,1)S(1)}, u32[]{:S(2)}, u32[]{:S(2)}) %collective-permute-start.5) | collective-permute-done | bytes 65568 | tf_op jit(solution)/shard_map/ppermute | solution.py:16
  48.4 6.3 %collective-permute-done.6 = bf16[4,64,128]{2,1,0:T(8,128)(2,1)S(1)} collective-permute-done((bf16[4,64,128]{2,1,0:T(8,128)(2,1)S(1)}, bf16[4,64,128]{2,1,0:T(8,128)(2,1)S(1)}, u32[]{:S(2)}, u32[]{:S(2)}) %collective-permute-start.6) | collective-permute-done | bytes 65568 | tf_op jit(solution)/shard_map/ppermute | solution.py:16
  56.2 207.7 %while.29 = (s32[]{:T(128)}, f32[4,512,4]{1,2,0:T(4,128)}, f32[4,512,4]{1,2,0:T(4,128)}, f32[4,512,128]{2,0,1:T(4,128)}, bf16[4,2048,128]{2,1,0:T(8,128)(2,1)}, ...) while((s32[]{:T(128)}, f32[4,512,4]{1,2,0:T(4,128)}, ...), condition=%wide.region_9.10_spmd, body=%wide.region_1.9_spmd.sunk | while | flops 148332544 | bytes 36866940 | solution.py:96
  60.1 36.4 %while.30 = (s32[]{:T(128)}, f32[4,512,4]{1,2,0:T(4,128)}, f32[4,512,4]{1,2,0:T(4,128)}, f32[4,512,128]{1,2,0:T(8,128)}, pred[4,512]{1,0:T(4,128)(4,1)S(1)}, /*i...) while((s32[]{:T(128)}, f32[4,512,4]{1,2,0:T(4,128)}, ...), condition=%wide.region_5.5_spmd, body=%wide.region_2.4_spmd.sunk | while | flops 147845120 | bytes 31656596 | solution.py:79
  83.4 3.2 %fusion.40 = f32[4,32,512]{2,1,0:T(8,128)S(1)} fusion(bf16[512,4,32]{0,2,1:T(8,128)(2,1)S(1)} %bitcast.125, f32[4,512,512]{2,1,0:T(8,128)} %copy-done.1, f32[4,512]{1,0:T(4,128)S(1)} %get-tuple-element.380, pred[512]{0:T(512)(128)(4,1)S(1)} %dynamic-slice_reduce_fusion.5), kind=kOutput, calls=%fused_computation.7.clone.1 | convolution fusion | flops 72351744 | bytes 4596224 | tf_op jit(solution)/shard_map/while/body/eval_jaxpr/while/body/eval_jaxpr/hck,khd->chd/dot_general | solution.py:71
  92.5 3.2 %fusion.40 = f32[4,32,512]{2,1,0:T(8,128)S(1)} fusion(bf16[512,4,32]{0,2,1:T(8,128)(2,1)S(1)} %bitcast.125, f32[4,512,512]{2,1,0:T(8,128)} %copy-done.1, f32[4,512]{1,0:T(4,128)S(1)} %get-tuple-element.380, pred[512]{0:T(512)(128)(4,1)S(1)} %dynamic-slice_reduce_fusion.5), kind=kOutput, calls=%fused_computation.7.clone.1 | convolution fusion | flops 72351744 | bytes 4596224 | tf_op jit(solution)/shard_map/while/body/eval_jaxpr/while/body/eval_jaxpr/hck,khd->chd/dot_general | solution.py:71
  100.2 7.9 %dynamic_update_slice.30 = f32[4,512,128]{2,0,1:T(4,128)} dynamic-update-slice(f32[4,512,128]{2,0,1:T(4,128)} %get-tuple-element.425, f32[1,512,128]{2,0,1:T(1,128)S(1)} %copy.96, s32[]{:T(128)S(6)} %copy.136, s32[]{:T(128)} %constant.86.clone.1..sunk, s32[]{:T(128)} %constant.86.clone.1..sunk) | dynamic-update-slice | bytes 524292 | tf_op jit(solution)/shard_map/while/body/jit(dynamic_update_index_in_dim)/dynamic_update_slice | solution.py:96
  112.0 36.4 %while.30 = (s32[]{:T(128)}, f32[4,512,4]{1,2,0:T(4,128)}, f32[4,512,4]{1,2,0:T(4,128)}, f32[4,512,128]{1,2,0:T(8,128)}, pred[4,512]{1,0:T(4,128)(4,1)S(1)}, /*i...) while((s32[]{:T(128)}, f32[4,512,4]{1,2,0:T(4,128)}, ...), condition=%wide.region_5.5_spmd, body=%wide.region_2.4_spmd.sunk | while | flops 147845120 | bytes 31656596 | solution.py:79
  152.1 7.9 %dynamic_update_slice.30 = f32[4,512,128]{2,0,1:T(4,128)} dynamic-update-slice(f32[4,512,128]{2,0,1:T(4,128)} %get-tuple-element.425, f32[1,512,128]{2,0,1:T(1,128)S(1)} %copy.96, s32[]{:T(128)S(6)} %copy.136, s32[]{:T(128)} %constant.86.clone.1..sunk, s32[]{:T(128)} %constant.86.clone.1..sunk) | dynamic-update-slice | bytes 524292 | tf_op jit(solution)/shard_map/while/body/jit(dynamic_update_index_in_dim)/dynamic_update_slice | solution.py:96
  163.9 36.4 %while.30 = (s32[]{:T(128)}, f32[4,512,4]{1,2,0:T(4,128)}, f32[4,512,4]{1,2,0:T(4,128)}, f32[4,512,128]{1,2,0:T(8,128)}, pred[4,512]{1,0:T(4,128)(4,1)S(1)}, /*i...) while((s32[]{:T(128)}, f32[4,512,4]{1,2,0:T(4,128)}, ...), condition=%wide.region_5.5_spmd, body=%wide.region_2.4_spmd.sunk | while | flops 147845120 | bytes 31656596 | solution.py:79
  187.2 3.2 %fusion.40 = f32[4,32,512]{2,1,0:T(8,128)S(1)} fusion(bf16[512,4,32]{0,2,1:T(8,128)(2,1)S(1)} %bitcast.125, f32[4,512,512]{2,1,0:T(8,128)} %copy-done.1, f32[4,512]{1,0:T(4,128)S(1)} %get-tuple-element.380, pred[512]{0:T(512)(128)(4,1)S(1)} %dynamic-slice_reduce_fusion.5), kind=kOutput, calls=%fused_computation.7.clone.1 | convolution fusion | flops 72351744 | bytes 4596224 | tf_op jit(solution)/shard_map/while/body/eval_jaxpr/while/body/eval_jaxpr/hck,khd->chd/dot_general | solution.py:71
  204.0 7.9 %dynamic_update_slice.30 = f32[4,512,128]{2,0,1:T(4,128)} dynamic-update-slice(f32[4,512,128]{2,0,1:T(4,128)} %get-tuple-element.425, f32[1,512,128]{2,0,1:T(1,128)S(1)} %copy.96, s32[]{:T(128)S(6)} %copy.136, s32[]{:T(128)} %constant.86.clone.1..sunk, s32[]{:T(128)} %constant.86.clone.1..sunk) | dynamic-update-slice | bytes 524292 | tf_op jit(solution)/shard_map/while/body/jit(dynamic_update_index_in_dim)/dynamic_update_slice | solution.py:96
  215.9 36.4 %while.30 = (s32[]{:T(128)}, f32[4,512,4]{1,2,0:T(4,128)}, f32[4,512,4]{1,2,0:T(4,128)}, f32[4,512,128]{1,2,0:T(8,128)}, pred[4,512]{1,0:T(4,128)(4,1)S(1)}, /*i...) while((s32[]{:T(128)}, f32[4,512,4]{1,2,0:T(4,128)}, ...), condition=%wide.region_5.5_spmd, body=%wide.region_2.4_spmd.sunk | while | flops 147845120 | bytes 31656596 | solution.py:79
  255.9 7.9 %dynamic_update_slice.30 = f32[4,512,128]{2,0,1:T(4,128)} dynamic-update-slice(f32[4,512,128]{2,0,1:T(4,128)} %get-tuple-element.425, f32[1,512,128]{2,0,1:T(1,128)S(1)} %copy.96, s32[]{:T(128)S(6)} %copy.136, s32[]{:T(128)} %constant.86.clone.1..sunk, s32[]{:T(128)} %constant.86.clone.1..sunk) | dynamic-update-slice | bytes 524292 | tf_op jit(solution)/shard_map/while/body/jit(dynamic_update_index_in_dim)/dynamic_update_slice | solution.py:96
  269.0 3.3 %all-to-all-start.2 = ((f32[8,1,1024]{2,1,0:T(1,128)}), f32[8,1,1024]{2,1,0:T(1,128)S(1)}, u32[]{:S(2)}, u32[]{:S(2)}) async-start(f32[8,1,1024]{2,1,0:T(1,128)} %reshape.121), calls=%async_computation.2 | async-start | bytes 65536 | tf_op jit(solution)/shard_map/all_to_all | solution.py:99
  279.0 9.7 %all_to_all.51 = f32[8,1,1024]{2,1,0:T(1,128)S(1)} all-to-all(f32[8,1,1024]{2,1,0:T(1,128)S(1)} %reshape.119), channel_id=1, replica_groups=mesh['dp'=4,'hist'=8] {'hist'}, dimensions={0} | all-to-all | bytes 65536 | tf_op jit(solution)/shard_map/all_to_all | solution.py:98
  288.7 4.4 %all-to-all-start = ((f32[1,4,512,128]{3,1,0,2:T(4,128)}), f32[1,4,512,128]{3,1,0,2:T(4,128)}, u32[]{:S(2)}, u32[]{:S(2)}) async-start(f32[1,4,512,128]{3,1,0,2:T(4,128)} %bitcast.136), calls=%async_computation | async-start | bytes 2097152 | tf_op jit(solution)/shard_map/all_to_all | solution.py:100
  307.5 4.2 %all-to-all-done = f32[1,4,512,128]{3,1,0,2:T(4,128)} async-done(((f32[1,4,512,128]{3,1,0,2:T(4,128)}), f32[1,4,512,128]{3,1,0,2:T(4,128)}, u32[]{:S(2)}, u32[]{:S(2)}) %all-to-all-start) | async-done | bytes 1048608 | tf_op jit(solution)/shard_map/all_to_all | solution.py:100
  (318 shorter events, 204.8 us)
Async XLA Ops:
  0.0 10.2 %copy-start = (bf16[4,2048,128]{2,1,0:T(8,128)(2,1)S(1)}, bf16[4,2048,128]{2,1,0:T(8,128)(2,1)}, u32[]{:S(2)}) copy-start(bf16[4,2048,128]{2,1,0:T(8,128)(2,1)} %param.10) | copy-start | bytes 6291460
  0.0 8.6 %collective-permute-start = (bf16[4,64,128]{2,1,0:T(8,128)(2,1)}, bf16[4,64,128]{2,1,0:T(8,128)(2,1)S(1)}, u32[]{:S(2)}, u32[]{:S(2)}) collective-permute-start(bf16[4,64,128]{2,1,0:T(8,128)(2,1)} %param.9), channel_id=1, source_target_pairs={{0,1},{1,2},{2,3},{3,4},{4,5},{5,6},{6,7},{7,0},{8,9},{9,10},{10,1... | collective-permute-start | bytes 196616 | tf_op jit(solution)/shard_map/ppermute | solution.py:16
  8.6 46.4 %copy-start.2 = (bf16[4,128,128]{2,1,0:T(8,128)(2,1)}, bf16[4,128,128]{2,1,0:T(8,128)(2,1)S(1)}, u32[]{:S(2)}) copy-start(bf16[4,128,128]{2,1,0:T(8,128)(2,1)S(1)} %all_gather.3) | copy-start | bytes 393220
  8.6 11.2 %collective-permute-start.1 = (bf16[4,64,128]{2,1,0:T(8,128)(2,1)S(1)}, bf16[4,64,128]{2,1,0:T(8,128)(2,1)S(1)}, u32[]{:S(2)}, u32[]{:S(2)}) collective-permute-start(bf16[4,64,128]{2,1,0:T(8,128)(2,1)S(1)} %collective-permute-done), channel_id=1, source_target_pairs={{0,1},{1,2},{2,3},{3,4},{4,5},{5,6},{6,7},{7,0},{8,9},{9,10},{10,1... | collective-permute-start | bytes 196616 | tf_op jit(solution)/shard_map/ppermute | solution.py:16
  19.9 7.0 %collective-permute-start.2 = (bf16[4,64,128]{2,1,0:T(8,128)(2,1)S(1)}, bf16[4,64,128]{2,1,0:T(8,128)(2,1)S(1)}, u32[]{:S(2)}, u32[]{:S(2)}) collective-permute-start(bf16[4,64,128]{2,1,0:T(8,128)(2,1)S(1)} %collective-permute-done.1), channel_id=1, source_target_pairs={{0,1},{1,2},{2,3},{3,4},{4,5},{5,6},{6,7},{7,0},{8,9},{9,10},{10,1... | collective-permute-start | bytes 196616 | tf_op jit(solution)/shard_map/ppermute | solution.py:16
  21.4 12.4 %copy-start.5 = (s32[4,64]{1,0:T(4,128)S(1)}, s32[4,64]{1,0:T(4,128)}, u32[]{:S(2)}) copy-start(s32[4,64]{1,0:T(4,128)} %param.13) | copy-start | bytes 3076
  21.4 26.3 %copy-start.6 = (s32[4]{0:T(128)S(1)}, s32[4]{0:T(128)}, u32[]{:S(2)}) copy-start(s32[4]{0:T(128)} %param.12) | copy-start | bytes 52
  21.4 33.4 %copy-start.3 = (bf16[4,64,128]{2,1,0:T(8,128)(2,1)S(1)}, bf16[4,64,128]{2,1,0:T(8,128)(2,1)}, u32[]{:S(2)}) copy-start(bf16[4,64,128]{2,1,0:T(8,128)(2,1)} %param.9) | copy-start | bytes 196612
  26.8 7.0 %collective-permute-start.3 = (bf16[4,64,128]{2,1,0:T(8,128)(2,1)S(1)}, bf16[4,64,128]{2,1,0:T(8,128)(2,1)S(1)}, u32[]{:S(2)}, u32[]{:S(2)}) collective-permute-start(bf16[4,64,128]{2,1,0:T(8,128)(2,1)S(1)} %collective-permute-done.2), channel_id=1, source_target_pairs={{0,1},{1,2},{2,3},{3,4},{4,5},{5,6},{6,7},{7,0},{8,9},{9,10},{10,1... | collective-permute-start | bytes 196616 | tf_op jit(solution)/shard_map/ppermute | solution.py:16
  33.8 7.0 %collective-permute-start.4 = (bf16[4,64,128]{2,1,0:T(8,128)(2,1)S(1)}, bf16[4,64,128]{2,1,0:T(8,128)(2,1)S(1)}, u32[]{:S(2)}, u32[]{:S(2)}) collective-permute-start(bf16[4,64,128]{2,1,0:T(8,128)(2,1)S(1)} %collective-permute-done.3), channel_id=1, source_target_pairs={{0,1},{1,2},{2,3},{3,4},{4,5},{5,6},{6,7},{7,0},{8,9},{9,10},{10,1... | collective-permute-start | bytes 196616 | tf_op jit(solution)/shard_map/ppermute | solution.py:16
  40.7 7.0 %collective-permute-start.5 = (bf16[4,64,128]{2,1,0:T(8,128)(2,1)S(1)}, bf16[4,64,128]{2,1,0:T(8,128)(2,1)S(1)}, u32[]{:S(2)}, u32[]{:S(2)}) collective-permute-start(bf16[4,64,128]{2,1,0:T(8,128)(2,1)S(1)} %collective-permute-done.4), channel_id=1, source_target_pairs={{0,1},{1,2},{2,3},{3,4},{4,5},{5,6},{6,7},{7,0},{8,9},{9,10},{10,1... | collective-permute-start | bytes 196616 | tf_op jit(solution)/shard_map/ppermute | solution.py:16
  47.7 7.0 %collective-permute-start.6 = (bf16[4,64,128]{2,1,0:T(8,128)(2,1)S(1)}, bf16[4,64,128]{2,1,0:T(8,128)(2,1)S(1)}, u32[]{:S(2)}, u32[]{:S(2)}) collective-permute-start(bf16[4,64,128]{2,1,0:T(8,128)(2,1)S(1)} %collective-permute-done.5), channel_id=1, source_target_pairs={{0,1},{1,2},{2,3},{3,4},{4,5},{5,6},{6,7},{7,0},{8,9},{9,10},{10,1... | collective-permute-start | bytes 196616 | tf_op jit(solution)/shard_map/ppermute | solution.py:16
  61.4 1.9 copy-start.1
  70.5 1.9 copy-start.1
  88.7 1.9 copy-start.1
  113.3 1.9 copy-start.1
  131.5 1.9 copy-start.1
  174.3 1.9 copy-start.1
  192.5 1.9 copy-start.1
  217.2 1.9 copy-start.1
  235.3 1.9 copy-start.1
  263.8 8.5 %copy-start.4 = (f32[4,512,4]{1,2,0:T(4,128)S(1)}, f32[4,512,4]{1,2,0:T(4,128)}, u32[]{:S(2)}) copy-start(f32[4,512,4]{1,2,0:T(4,128)} %get-tuple-element.94) | copy-start | bytes 98308
  269.0 10.0 %all-to-all-start.2 = ((f32[8,1,1024]{2,1,0:T(1,128)}), f32[8,1,1024]{2,1,0:T(1,128)S(1)}, u32[]{:S(2)}, u32[]{:S(2)}) async-start(f32[8,1,1024]{2,1,0:T(1,128)} %reshape.121), calls=%async_computation.2 | async-start | bytes 65536 | tf_op jit(solution)/shard_map/all_to_all | solution.py:99
  288.7 23.0 %all-to-all-start = ((f32[1,4,512,128]{3,1,0,2:T(4,128)}), f32[1,4,512,128]{3,1,0,2:T(4,128)}, u32[]{:S(2)}, u32[]{:S(2)}) async-start(f32[1,4,512,128]{3,1,0,2:T(4,128)} %bitcast.136), calls=%async_computation | async-start | bytes 2097152 | tf_op jit(solution)/shard_map/all_to_all | solution.py:100
  (7 other events, 13.5 us)
